TPU v7x, 256 devices: a 4x2x16 block of a 4x16x16 slice. The times are simulated.
256 devices in a mesh: parts: 2 (over y), row: 16 (over z), chan: 4 (over x), sub: 2 (over core).
Axes of the slice: x: 4, y: 2, z: 16, core: 2. Of those that a mesh axis runs over, the one named last changes fastest.
The devices are a block of a 4x16x16 slice.
Arguments:
- pair: bfloat16 [896, 448, 128], P(('parts', 'row', 'sub'), 'chan'), parts along dimension 0, may hold values from -6 to 6
- pair_mask: int32 [896, 448], P(('parts', 'row', 'sub'), 'chan'), parts along dimension 0, may hold values 0 or 1
- out_in_gain: float32 [128], replicated, may hold values from 0.5 to 1.5
- out_proj: bfloat16 [128, 640], replicated, may hold values from -0.5 to 0.5
- out_mid_gain: float32 [128], replicated, may hold values from 0.5 to 1.5
- out_final: bfloat16 [128, 128], replicated, may hold values from -0.5 to 0.5
- in_in_gain: float32 [128], replicated, may hold values from 0.5 to 1.5
- in_proj: bfloat16 [128, 640], replicated, may hold values from -0.5 to 0.5
- in_mid_gain: float32 [128], replicated, may hold values from 0.5 to 1.5
- in_final: bfloat16 [128, 128], replicated, may hold values from -0.5 to 0.5
Outputs:
- updated: bfloat16 [896, 448, 128], P(('parts', 'row', 'sub'), 'chan'), parts along dimension 0
There are 2 independent parts, one for each index of `parts`. A program takes and returns all parts, laid end to end along the dimension named above; an argument that names none is the same for every part. Nothing has to cross between parts.
All inputs are finite; a program needn't handle non-finite values. No bound on the sum of `pair_mask` on one device may be relied on, other than what follows from the above.
Results may differ from a plain program's by a relative error of at most 0.014.
Values may be sent and summed in bfloat16 or wider, within the bound.
No kernel may reach another device: no remote copies, remote signals or barrier semaphores. Data moves between devices by JAX's collectives and lax.ppermute only.
A program may use at most 64 MiB of HBM per device.

v0:
```python
import jax
import jax.numpy as jnp
from jax import lax
from jax.sharding import PartitionSpec as P


def norm_last(values, gain):
    mean = jnp.mean(values, axis=-1, keepdims=True)
    var = jnp.mean((values - mean) ** 2, axis=-1, keepdims=True)
    return (values - mean) / jnp.sqrt(var + 1e-05) * gain


def norm_first(values, gain):
    mean = jnp.mean(values, axis=0, keepdims=True)
    var = jnp.mean((values - mean) ** 2, axis=0, keepdims=True)
    return (values - mean) / jnp.sqrt(var + 1e-05) * gain[:, None, None]


def project(pair, pair_mask, in_gain, proj, left_form, right_form, left_across):
    hidden = (proj.shape[1] - pair.shape[2]) // 4
    normed = norm_last(pair.astype(jnp.float32), in_gain).astype(jnp.bfloat16)
    keep = pair_mask.astype(jnp.float32)
    left_raw = jnp.einsum(
        left_form, normed, proj[:, : 2 * hidden], preferred_element_type=jnp.float32
    )
    right_raw = jnp.einsum(
        right_form, normed, proj[:, 2 * hidden : 4 * hidden], preferred_element_type=jnp.float32
    )
    left_keep = keep.T[None] if left_across else keep[None]
    left = (jax.nn.sigmoid(left_raw[:hidden]) * left_raw[hidden:] * left_keep).astype(jnp.bfloat16)
    right = (jax.nn.sigmoid(right_raw[:hidden]) * right_raw[hidden:] * keep[None]).astype(
        jnp.bfloat16
    )
    gate = jax.nn.sigmoid(
        jnp.dot(normed, proj[:, 4 * hidden :], preferred_element_type=jnp.float32)
    )
    return (left, right, gate)


def finish(pair, product, gate, mid_gain, final):
    whole = lax.all_to_all(
        product.astype(jnp.bfloat16), "chan", split_axis=2, concat_axis=0, tiled=True
    ).astype(product.dtype)
    normed = norm_first(whole, mid_gain).astype(jnp.bfloat16)
    update = jnp.einsum("crq,cd->rqd", normed, final, preferred_element_type=jnp.float32)
    return (pair.astype(jnp.float32) + gate * update).astype(jnp.bfloat16)


def shards(
    pair,
    pair_mask,
    out_in_gain,
    out_proj,
    out_mid_gain,
    out_final,
    in_in_gain,
    in_proj,
    in_mid_gain,
    in_final,
):
    left, right, gate = project(
        pair, pair_mask, out_in_gain, out_proj, "rqd,de->erq", "rqd,de->erq", False
    )
    left, right = (
        lax.all_to_all(left, "chan", split_axis=0, concat_axis=2, tiled=True),
        lax.all_to_all(right, "chan", split_axis=0, concat_axis=2, tiled=True),
    )
    product = jnp.einsum(
        "cik,cjk->cij",
        left,
        lax.all_gather(right, ("row", "sub"), axis=1, tiled=True),
        preferred_element_type=jnp.float32,
    )
    middle = finish(pair, product, gate, out_mid_gain, out_final)
    left_in, right_in, gate_in = project(
        middle, pair_mask, in_in_gain, in_proj, "rqd,de->eqr", "rqd,de->erq", True
    )
    columns = lax.all_to_all(
        lax.all_to_all(left_in, "chan", split_axis=0, concat_axis=1, tiled=True),
        ("row", "sub"),
        split_axis=1,
        concat_axis=2,
        tiled=True,
    )
    right_in = lax.all_to_all(right_in, "chan", split_axis=0, concat_axis=2, tiled=True)
    product_in = jnp.einsum(
        "cik,ckj->cij",
        columns,
        lax.all_gather(right_in, ("row", "sub"), axis=1, tiled=True),
        preferred_element_type=jnp.float32,
    )
    return finish(middle, product_in, gate_in, in_mid_gain, in_final)


def solution(mesh):
    placed = (
        P(("parts", "row", "sub"), "chan", None),
        P(("parts", "row", "sub"), "chan"),
        P(),
        P(),
        P(),
        P(),
        P(),
        P(),
        P(),
        P(),
    )
    return jax.shard_map(
        shards,
        mesh=mesh,
        in_specs=placed,
        out_specs=P(("parts", "row", "sub"), "chan", None),
        check_vma=False,
    )
```

profile of v0, /device:TPU:33, one launch (start us, length us, event | category | flops | bytes accessed | tf_op | source)
XLA Modules:
  0.0 357.3 jit_solution(9563343300795367324)
XLA Ops:
  6.6 1.2 convert_reduce_fusion
  7.8 1.5 fusion.29
  9.4 1.7 convolution_bitcast_fusion.2
  11.1 1.4 convolution_bitcast_fusion.3
  13.5 11.9 %all_to_all.108 = bf16[128,14,112]{2,1,0:T(8,128)(2,1)S(1)} all-to-all(bf16[128,14,112]{2,1,0:T(8,128)(2,1)S(1)} %copy.93), channel_id=1, replica_groups=mesh['parts'=2,'row'=16,'chan'=4,'sub'=2] {'chan'}, dimensions={0} | all-to-all | bytes 802816 | tf_op jit(solution)/shard_map/all_to_all | solution.py:66
  27.3 9.4 %all_to_all.109 = bf16[128,14,112]{2,1,0:T(8,128)(2,1)S(1)} all-to-all(bf16[128,14,112]{2,1,0:T(8,128)(2,1)S(1)} %copy.90), channel_id=1, replica_groups=mesh['parts'=2,'row'=16,'chan'=4,'sub'=2] {'chan'}, dimensions={0} | all-to-all | bytes 802816 | tf_op jit(solution)/shard_map/all_to_all | solution.py:65
  37.5 98.7 %all-gather.3.cloned.1.call-done = bf16[32,448,448]{2,0,1:T(8,128)(2,1)} async-done(((bf16[32,14,448]{2,0,1:T(8,128)(2,1)}), bf16[32,448,448]{2,0,1:T(8,128)(2,1)}) %all-gather.3.cloned.1.call-update) | async-done | bytes 12845072 | tf_op jit(solution)/shard_map/all_gather | solution.py:71
  136.2 26.0 %fusion.12 = bf16[32,14,448]{2,1,0:T(8,128)(2,1)S(1)} fusion(bf16[32,14,448]{2,1,0:T(8,128)(2,1)S(1)} %reshape.80, bf16[32,448,448]{2,0,1:T(8,128)(2,1)} %all-gather.3.cloned.1.call-done), kind=kOutput, calls=%fused_computation.20 | convolution fusion | flops 180031488 | bytes 13647872 | tf_op jit(solution)/shard_map/cik,cjk->cij/dot_general | solution.py:68
  162.2 2.0 copy.98
  164.2 2.1 reshape.82
  166.4 4.0 %all-to-all-start.2 = ((bf16[4,2,25088]{2,1,0:T(2,128)(2,1)}), bf16[4,2,25088]{2,1,0:T(2,128)(2,1)S(1)}, u32[]{:S(2)}, u32[]{:S(2)}) async-start(bf16[4,2,25088]{2,1,0:T(2,128)(2,1)} %reshape.82), calls=%async_computation.2 | async-start | bytes 802816 | tf_op jit(solution)/shard_map/all_to_all | solution.py:41
  170.4 1.4 fusion.11
  171.8 6.3 %all-to-all-done.2 = bf16[4,2,25088]{2,1,0:T(2,128)(2,1)S(1)} async-done(((bf16[4,2,25088]{2,1,0:T(2,128)(2,1)}), bf16[4,2,25088]{2,1,0:T(2,128)(2,1)S(1)}, u32[]{:S(2)}, u32[]{:S(2)}) %all-to-all-start.2) | async-done | bytes 401440 | tf_op jit(solution)/shard_map/all_to_all | solution.py:41
  178.1 1.4 reshape.83
  179.5 1.6 copy.99
  185.4 10.3 %all_to_all.110 = bf16[128,14,112]{2,1,0:T(8,128)(2,1)S(1)} all-to-all(bf16[128,14,112]{2,1,0:T(8,128)(2,1)S(1)} %copy.108), channel_id=1, replica_groups=mesh['parts'=2,'row'=16,'chan'=4,'sub'=2] {'chan'}, dimensions={0} | all-to-all | bytes 802816 | tf_op jit(solution)/shard_map/all_to_all | solution.py:85
  198.3 9.4 %all_to_all.111 = bf16[128,112,14]{1,2,0:T(8,128)(2,1)S(1)} all-to-all(bf16[128,112,14]{1,2,0:T(8,128)(2,1)S(1)} %copy.102), channel_id=1, replica_groups=mesh['parts'=2,'row'=16,'chan'=4,'sub'=2] {'chan'}, dimensions={0} | all-to-all | bytes 802816 | tf_op jit(solution)/shard_map/all_to_all | solution.py:79
  207.6 1.6 copy.123
  209.3 1.4 reshape.84
  210.7 45.8 %all_to_all.112 = bf16[32,2,3136]{2,1,0:T(2,128)(2,1)S(1)} all-to-all(bf16[32,2,3136]{2,1,0:T(2,128)(2,1)S(1)} %reshape.84), channel_id=1, replica_groups=mesh['parts'=2,'row'=16,'chan'=4,'sub'=2] {'row','sub'}, dimensions={0} | all-to-all | bytes 802816 | tf_op jit(solution)/shard_map/all_to_all | solution.py:78
  256.5 1.7 reshape.85
  258.2 4.7 %copy.126 = bf16[32,14,32,14]{3,2,1,0:T(8,128)(2,1)} copy(bf16[32,14,32,14]{0,3,1,2:T(8,128)(2,1)S(1)} %bitcast.105) | data formatting | bytes 802816 | tf_op jit(solution)/shard_map/all_to_all | solution.py:78
  262.9 7.3 %reshape.81 = bf16[32,14,448]{2,1,0:T(8,128)(2,1)S(1)} reshape(bf16[32,14,32,14]{3,2,1,0:T(8,128)(2,1)} %copy.126) | data formatting | bytes 802816 | tf_op jit(solution)/shard_map/all_to_all | solution.py:78
  270.2 37.5 %all-gather.5.cloned.1.call-done = bf16[32,448,448]{2,0,1:T(8,128)(2,1)} async-done(((bf16[32,14,448]{2,0,1:T(8,128)(2,1)}), bf16[32,448,448]{2,0,1:T(8,128)(2,1)}) %all-gather.5.cloned.1.call-update) | async-done | bytes 12845072 | tf_op jit(solution)/shard_map/all_gather | solution.py:89
  307.7 20.7 %fusion.15 = bf16[32,14,448]{2,1,0:T(8,128)(2,1)S(1)} fusion(bf16[32,14,448]{2,1,0:T(8,128)(2,1)S(1)} %reshape.81, bf16[32,448,448]{2,0,1:T(8,128)(2,1)} %all-gather.5.cloned.1.call-done), kind=kOutput, calls=%fused_computation.21 | convolution fusion | flops 180031488 | bytes 13647872 | tf_op jit(solution)/shard_map/cik,ckj->cij/dot_general | solution.py:86
  328.4 1.6 copy.113
  330.0 2.1 reshape.86
  332.1 4.0 %all-to-all-start.6 = ((bf16[4,2,25088]{2,1,0:T(2,128)(2,1)}), bf16[4,2,25088]{2,1,0:T(2,128)(2,1)S(1)}, u32[]{:S(2)}, u32[]{:S(2)}) async-start(bf16[4,2,25088]{2,1,0:T(2,128)(2,1)} %reshape.86), calls=%async_computation.6 | async-start | bytes 802816 | tf_op jit(solution)/shard_map/all_to_all | solution.py:41
  336.1 2.0 fusion.7
  338.1 5.7 %all-to-all-done.6 = bf16[4,2,25088]{2,1,0:T(2,128)(2,1)S(1)} async-done(((bf16[4,2,25088]{2,1,0:T(2,128)(2,1)}), bf16[4,2,25088]{2,1,0:T(2,128)(2,1)S(1)}, u32[]{:S(2)}, u32[]{:S(2)}) %all-to-all-start.6) | async-done | bytes 401440 | tf_op jit(solution)/shard_map/all_to_all | solution.py:41
  343.8 1.4 reshape.87
  345.2 1.6 copy.114
  (74 shorter events, 13.5 us)
Async XLA Ops:
  6.5 176.1 %copy-start = (bf16[128,128]{1,0:T(8,128)(2,1)S(1)}, bf16[128,128]{1,0:T(8,128)(2,1)}, u32[]{:S(2)}) copy-start(bf16[128,128]{1,0:T(8,128)(2,1)} %param.15) | copy-start | bytes 98308
  6.6 129.7 %all-gather.3.cloned.1.call-start = ((), (), s32[]{:S(2)}) async-start(), calls=%async_computation.7 | async-start | bytes 15138816 | tf_op jit(solution)/shard_map/all_gather | solution.py:71
  9.3 1.7 copy-start.2
  9.3 1.7 copy-start.14
  9.4 3.2 copy-start.9
  11.1 1.5 copy-start.8
  164.2 6.2 %copy-start.10 = (f32[14,112]{1,0:T(8,128)S(1)}, f32[14,112]{1,0:T(8,128)}, u32[]{:S(2)}) copy-start(f32[14,112]{1,0:T(8,128)} %copy-done.9) | copy-start | bytes 18820
  164.2 6.1 %copy-start.15 = (f32[128]{0:T(128)S(1)}, f32[128]{0:T(128)}, u32[]{:S(2)}) copy-start(f32[128]{0:T(128)} %param.12) | copy-start | bytes 1540
  166.4 11.7 %all-to-all-start.2 = ((bf16[4,2,25088]{2,1,0:T(2,128)(2,1)}), bf16[4,2,25088]{2,1,0:T(2,128)(2,1)S(1)}, u32[]{:S(2)}, u32[]{:S(2)}) async-start(bf16[4,2,25088]{2,1,0:T(2,128)(2,1)} %reshape.82), calls=%async_computation.2 | async-start | bytes 802816 | tf_op jit(solution)/shard_map/all_to_all | solution.py:41
  170.4 137.3 %all-gather.5.cloned.1.call-start = ((), (), s32[]{:S(2)}) async-start(), calls=%async_computation.8 | async-start | bytes 15138816 | tf_op jit(solution)/shard_map/all_gather | solution.py:89
  181.8 0.7 copy-start.11
  182.6 1.1 copy-start.13
  182.6 1.6 copy-start.6
  184.3 12.9 %copy-start.3 = (bf16[14,112,128]{2,1,0:T(8,128)(2,1)}, bf16[14,112,128]{2,1,0:T(8,128)(2,1)S(1)}, u32[]{:S(2)}) copy-start(bf16[14,112,128]{2,1,0:T(8,128)(2,1)S(1)} %multiply_convert_fusion) | copy-start | bytes 1204228
  329.9 6.1 %copy-start.4 = (bf16[14,112,128]{2,1,0:T(8,128)(2,1)S(1)}, bf16[14,112,128]{2,1,0:T(8,128)(2,1)}, u32[]{:S(2)}) copy-start(bf16[14,112,128]{2,1,0:T(8,128)(2,1)} %copy-done.3) | copy-start | bytes 1204228
  332.1 11.7 %all-to-all-start.6 = ((bf16[4,2,25088]{2,1,0:T(2,128)(2,1)}), bf16[4,2,25088]{2,1,0:T(2,128)(2,1)S(1)}, u32[]{:S(2)}, u32[]{:S(2)}) async-start(bf16[4,2,25088]{2,1,0:T(2,128)(2,1)} %reshape.86), calls=%async_computation.6 | async-start | bytes 802816 | tf_op jit(solution)/shard_map/all_to_all | solution.py:41
  347.5 0.7 copy-start.12
  348.0 1.1 copy-start.5
  348.0 1.1 copy-start.7
  348.0 2.2 copy-start.1
Sparse Core Ops, SparseCore 0:
  27.0 109.2 all-gather.2
  197.3 110.3 all-gather.4
where the time goes:
time: 362 us; the launch traced here: 357 us
  waiting for transfers between devices  148 us (41%)
  blocking collectives  86.7 us (24%)
  matrix products  55.5 us (15%)
  local copies, waits for them, and re-layouts  38.5 us (11%)
  between operations  14.2 us (4%)
  starting transfers between devices  7.98 us (2%)
  other arithmetic  6.1 us (2%)
    all_gather x1, waiting for transfers between devices, shards(): lax.all_gather(right, ('row', 'sub'), axis=1, tiled=True)  98.7 us
    all_to_all x1, blocking collectives, shards(): lax.all_to_all(lax.all_to_all(left_in, 'chan', split_axis=0, concat_axis=...  45.8 us
    all_gather x1, waiting for transfers between devices, shards(): lax.all_gather(right_in, ('row', 'sub'), axis=1, tiled=True)  37.5 us
    dot_general x1, matrix products, shards(): jnp.einsum('cik,cjk->cij', left, lax.all_gather(right, ('row', 'sub'), ax...  26 us
    dot_general x1, matrix products, shards(): jnp.einsum('cik,ckj->cij', columns, lax.all_gather(right_in, ('row', 'sub...  20.7 us
    all_to_all x2, local copies, waits for them, and re-layouts, shards(): lax.all_to_all(lax.all_to_all(left_in, 'chan', split_axis=0, concat_axis=...  12 us
    all_to_all x2, waiting for transfers between devices, finish(): lax.all_to_all(product.astype(jnp.bfloat16), 'chan', split_axis=2, concat...  12 us
    all_to_all x1, blocking collectives, shards(): lax.all_to_all(right, 'chan', split_axis=0, concat_axis=2, tiled=True)  11.9 us
  transfers between devices with their start and end apart: 4, of which 4 were waited for; matrix products, arithmetic and copies ran while one was open for 6% of the time, Pallas kernels for 0%

commit v1 on v0

v1 whole, which is shorter than its diff:
```python
import jax
import jax.numpy as jnp
from jax import lax
from jax.sharding import PartitionSpec as P

GROUP = ("chan", "row", "sub")


def norm(values, gain, axis):
    mean = jnp.mean(values, axis=axis, keepdims=True)
    var = jnp.mean((values - mean) ** 2, axis=axis, keepdims=True)
    return (values - mean) / jnp.sqrt(var + 1e-05) * gain


def exchange(values):
    return lax.all_to_all(values, GROUP, split_axis=0, concat_axis=0, tiled=True)


def slabs(pairs, keep, in_gain, proj):
    channels = pairs.shape[1]
    hidden = (proj.shape[1] - channels) // 4
    normed = norm(pairs.astype(jnp.float32), in_gain, 1).astype(jnp.bfloat16)
    raw = jnp.einsum("de,pd->ep", proj[:, : 4 * hidden], normed, preferred_element_type=jnp.float32)
    left = jax.nn.sigmoid(raw[:hidden]) * raw[hidden : 2 * hidden] * keep[None]
    right = jax.nn.sigmoid(raw[2 * hidden : 3 * hidden]) * raw[3 * hidden :] * keep[None]
    gate = jax.nn.sigmoid(
        jnp.dot(normed, proj[:, 4 * hidden :], preferred_element_type=jnp.float32)
    )
    return jnp.stack([left.astype(jnp.bfloat16), right.astype(jnp.bfloat16)], 1), gate


def update(pairs, keep, in_gain, proj, mid_gain, final, incoming, rows, cols, chans):
    both, gate = slabs(pairs, keep, in_gain, proj)
    got = exchange(both)
    size = got.shape[0]
    planes = got.reshape(chans, size // chans, 2, rows, cols)
    planes = planes.transpose(2, 1, 3, 0, 4).reshape(2, size // chans * rows, chans * cols)
    product = jnp.einsum(
        "ki,kj->ij" if incoming else "ik,jk->ij",
        planes[0],
        planes[1],
        preferred_element_type=jnp.float32,
    ).astype(jnp.bfloat16)
    parts = product.reshape(size // chans, rows, chans, cols).transpose(2, 0, 1, 3)
    whole = exchange(parts.reshape(size, 2, rows * cols // 2)).reshape(size, rows * cols)
    normed = norm(whole.astype(jnp.float32), mid_gain[:, None], 0).astype(jnp.bfloat16)
    change = jnp.einsum("cp,cd->pd", normed, final, preferred_element_type=jnp.float32)
    return (pairs.astype(jnp.float32) + gate * change).astype(jnp.bfloat16)


def solution(mesh):
    chans = mesh.shape["chan"]

    def shards(
        pair,
        pair_mask,
        out_in_gain,
        out_proj,
        out_mid_gain,
        out_final,
        in_in_gain,
        in_proj,
        in_mid_gain,
        in_final,
    ):
        rows, cols, channels = pair.shape
        pairs = pair.reshape(rows * cols, channels)
        keep = pair_mask.astype(jnp.float32).reshape(rows * cols)
        middle = update(
            pairs, keep, out_in_gain, out_proj, out_mid_gain, out_final, False, rows, cols, chans
        )
        updated = update(
            middle, keep, in_in_gain, in_proj, in_mid_gain, in_final, True, rows, cols, chans
        )
        return updated.reshape(rows, cols, channels)

    placed = (
        P(("parts", "row", "sub"), "chan", None),
        P(("parts", "row", "sub"), "chan"),
    ) + (P(),) * 8
    return jax.shard_map(
        shards,
        mesh=mesh,
        in_specs=placed,
        out_specs=P(("parts", "row", "sub"), "chan", None),
        check_vma=False,
    )
```

time: 362 us -> 241 us (0.67); the launches traced: 357 us -> 240 us
  waiting for transfers between devices: 148 us -> 58 us
  matrix products: 55.5 us -> 6.19 us
  blocking collectives: 86.7 us -> 130 us
  local copies, waits for them, and re-layouts: 38.5 us -> 14.8 us
  between operations: 14.2 us -> 0.4 us
  starting transfers between devices: 7.98 us -> 21.2 us
  other arithmetic: 6.1 us -> 9.72 us
    all_gather x2 -> x0, waiting for transfers between devices: 136 us -> none  [the longest x1 98.7 us: shards(): lax.all_gather(right, ('row', 'sub'), axis=1, tiled=True)]
    dot_general x10 -> x8, matrix products: 55.5 us -> 6.19 us  [the longest x2 2.1 us: slabs(): jnp.einsum('de,pd->ep', proj[:, :4 * hidden], normed, preferred_element_t...]
    all_to_all x2, waiting for transfers between devices: 12 us -> 58 us  [exchange(): lax.all_to_all(values, GROUP, split_axis=0, concat_axis=0, tiled=True)]
    all_to_all x5 -> x2, blocking collectives: 86.7 us -> 130 us  [exchange(): lax.all_to_all(values, GROUP, split_axis=0, concat_axis=0, tiled=True)]
    all_to_all x11 -> x0, local copies, waits for them, and re-layouts: 20.6 us -> none  [the longest x2 12 us: shards(): lax.all_to_all(lax.all_to_all(left_in, 'chan', split_axis=0, concat_axis=...]
    all_to_all x2, starting transfers between devices: 7.98 us -> 21.2 us  [exchange(): lax.all_to_all(values, GROUP, split_axis=0, concat_axis=0, tiled=True)]
    unnamed x38 -> x14, local copies, waits for them, and re-layouts: 11.2 us -> 0.04 us
    reshape x0 -> x10, local copies, waits for them, and re-layouts: none -> 7.45 us  [the longest x2 3.36 us: update(): parts.reshape(size, 2, rows * cols // 2)]
  transfers between devices with their start and end apart: 4 -> 2, of which waited for: 4 -> 2; matrix products, arithmetic and copies ran while one was open for 6% -> 1% of each run, Pallas kernels for 0% -> 0%
where the time goes in v1:
time: 241 us; the launch traced here: 240 us
  blocking collectives  130 us (54%)
  waiting for transfers between devices  58 us (24%)
  starting transfers between devices  21.2 us (9%)
  local copies, waits for them, and re-layouts  14.8 us (6%)
  other arithmetic  9.72 us (4%)
  matrix products  6.19 us (3%)
    all_to_all x2, blocking collectives, exchange(): lax.all_to_all(values, GROUP, split_axis=0, concat_axis=0, tiled=True)  130 us
    all_to_all x2, waiting for transfers between devices, exchange(): lax.all_to_all(values, GROUP, split_axis=0, concat_axis=0, tiled=True)  58 us
    all_to_all x2, starting transfers between devices, exchange(): lax.all_to_all(values, GROUP, split_axis=0, concat_axis=0, tiled=True)  21.2 us
  transfers between devices with their start and end apart: 2, of which 2 were waited for; matrix products, arithmetic and copies ran while one was open for 1% of the time, Pallas kernels for 0%

profile of v1, /device:TPU:33, one launch (start us, length us, event | category | flops | bytes accessed | tf_op | source)
XLA Modules:
  0.0 240.0 jit_solution(8881973482916927142)
XLA Ops:
  0.0 1.2 convert_reduce_fusion
  1.2 1.5 multiply_reduce_fusion.3
  2.9 0.7 convert_element_type.78
  3.7 1.5 fusion.39
  5.2 1.5 convolution_bitcast_fusion.1
  6.7 0.5 fusion.40
  7.2 1.3 copy.21
  8.5 75.9 %all_to_all.20 = bf16[128,2,1568]{2,1,0:T(2,128)(2,1)S(1)} all-to-all(bf16[128,2,1568]{2,1,0:T(2,128)(2,1)S(1)} %copy.21), channel_id=1, replica_groups=mesh['parts'=2,'row'=16,'chan'=4,'sub'=2] {'chan','row','sub'}, dimensions={0} | all-to-all | bytes 1605632 | tf_op jit(solution)/shard_map/all_to_all | solution.py:16
  84.5 1.5 reshape.163
  88.5 1.7 reshape.155
  90.2 10.6 %all-to-all-start.1 = ((bf16[128,2,784]{2,1,0:T(2,128)(2,1)}), bf16[128,2,784]{2,1,0:T(2,128)(2,1)S(1)}, u32[]{:S(2)}, u32[]{:S(2)}) async-start(bf16[128,2,784]{2,1,0:T(2,128)(2,1)} %reshape.155), calls=%async_computation.1 | async-start | bytes 917504 | tf_op jit(solution)/shard_map/all_to_all | solution.py:16
  100.8 1.2 fusion.7
  102.0 28.7 %all-to-all-done.1 = bf16[128,2,784]{2,1,0:T(2,128)(2,1)S(1)} async-done(((bf16[128,2,784]{2,1,0:T(2,128)(2,1)}), bf16[128,2,784]{2,1,0:T(2,128)(2,1)S(1)}, u32[]{:S(2)}, u32[]{:S(2)}) %all-to-all-start.1) | async-done | bytes 401440 | tf_op jit(solution)/shard_map/all_to_all | solution.py:16
  131.3 0.6 multiply_reduce_fusion.1
  132.0 0.6 copy.26
  132.6 0.5 fusion.36
  133.1 0.5 fusion.50
  133.6 0.5 multiply_reduce_fusion.2
  134.2 0.6 convolution_bitcast_fusion
  134.8 0.5 fusion.42
  135.4 1.3 copy.27
  136.6 53.8 %all_to_all.21 = bf16[128,2,1568]{2,1,0:T(2,128)(2,1)S(1)} all-to-all(bf16[128,2,1568]{2,1,0:T(2,128)(2,1)S(1)} %copy.27), channel_id=1, replica_groups=mesh['parts'=2,'row'=16,'chan'=4,'sub'=2] {'chan','row','sub'}, dimensions={0} | all-to-all | bytes 1605632 | tf_op jit(solution)/shard_map/all_to_all | solution.py:16
  190.5 1.5 reshape.164
  194.5 1.7 reshape.158
  196.2 10.5 %all-to-all-start.3 = ((bf16[128,2,784]{2,1,0:T(2,128)(2,1)}), bf16[128,2,784]{2,1,0:T(2,128)(2,1)S(1)}, u32[]{:S(2)}, u32[]{:S(2)}) async-start(bf16[128,2,784]{2,1,0:T(2,128)(2,1)} %reshape.158), calls=%async_computation.3 | async-start | bytes 917504 | tf_op jit(solution)/shard_map/all_to_all | solution.py:16
  206.7 0.6 fusion.4
  207.4 29.3 %all-to-all-done.3 = bf16[128,2,784]{2,1,0:T(2,128)(2,1)S(1)} async-done(((bf16[128,2,784]{2,1,0:T(2,128)(2,1)}), bf16[128,2,784]{2,1,0:T(2,128)(2,1)S(1)}, u32[]{:S(2)}, u32[]{:S(2)}) %all-to-all-start.3) | async-done | bytes 401440 | tf_op jit(solution)/shard_map/all_to_all | solution.py:16
  236.6 0.4 convert_reduce_fusion.1
  237.2 0.6 multiply_reduce_fusion
  237.9 0.6 copy.32
  238.5 0.5 fusion.33
  239.0 1.0 fusion.10
  (50 shorter events, 6.2 us)
Async XLA Ops:
  0.0 133.1 %copy-start = (bf16[128,128]{1,0:T(8,128)(2,1)S(1)}, bf16[128,128]{1,0:T(8,128)(2,1)}, u32[]{:S(2)}) copy-start(bf16[128,128]{1,0:T(8,128)(2,1)} %param.15) | copy-start | bytes 98308
  90.2 42.5 %copy-start.4 = (f32[128]{0:T(128)S(1)}, f32[128]{0:T(128)}, u32[]{:S(2)}) copy-start(f32[128]{0:T(128)} %param.14) | copy-start | bytes 1540
  90.2 40.6 %all-to-all-start.1 = ((bf16[128,2,784]{2,1,0:T(2,128)(2,1)}), bf16[128,2,784]{2,1,0:T(2,128)(2,1)S(1)}, u32[]{:S(2)}, u32[]{:S(2)}) async-start(bf16[128,2,784]{2,1,0:T(2,128)(2,1)} %reshape.155), calls=%async_computation.1 | async-start | bytes 917504 | tf_op jit(solution)/shard_map/all_to_all | solution.py:16
  100.8 32.3 %copy-start.1 = (bf16[14,112,128]{2,1,0:T(8,128)(2,1)S(1)}, bf16[14,112,128]{2,1,0:T(8,128)(2,1)}, u32[]{:S(2)}) copy-start(bf16[14,112,128]{2,1,0:T(8,128)(2,1)} %param.10) | copy-start | bytes 1204228
  131.2 3.0 %copy-start.2 = (bf16[128,640]{1,0:T(8,128)(2,1)S(1)}, bf16[128,640]{1,0:T(8,128)(2,1)}, u32[]{:S(2)}) copy-start(bf16[128,640]{1,0:T(8,128)(2,1)} %param.17) | copy-start | bytes 491524
  131.2 3.0 %copy-start.5 = (f32[128]{0:T(128)S(1)}, f32[128]{0:T(128)}, u32[]{:S(2)}) copy-start(f32[128]{0:T(128)} %param.16) | copy-start | bytes 1540
  196.2 40.4 %all-to-all-start.3 = ((bf16[128,2,784]{2,1,0:T(2,128)(2,1)}), bf16[128,2,784]{2,1,0:T(2,128)(2,1)S(1)}, u32[]{:S(2)}, u32[]{:S(2)}) async-start(bf16[128,2,784]{2,1,0:T(2,128)(2,1)} %reshape.158), calls=%async_computation.3 | async-start | bytes 917504 | tf_op jit(solution)/shard_map/all_to_all | solution.py:16
  206.7 31.8 %copy-start.6 = (f32[128]{0:T(128)S(1)}, f32[128]{0:T(128)}, u32[]{:S(2)}) copy-start(f32[128]{0:T(128)} %param.18) | copy-start | bytes 1540
  207.4 31.7 %copy-start.3 = (bf16[128,128]{1,0:T(8,128)(2,1)S(1)}, bf16[128,128]{1,0:T(8,128)(2,1)}, u32[]{:S(2)}) copy-start(bf16[128,128]{1,0:T(8,128)(2,1)} %param.19) | copy-start | bytes 98308

commit v2 on v1

v2 whole, which is shorter than its diff:
```python
import jax
import jax.numpy as jnp
from jax import lax
from jax.experimental import pallas as pl
from jax.experimental.pallas import tpu as pltpu
from jax.sharding import PartitionSpec as P

GROUP = ("row", "sub", "chan")


def exchange(values):
    return lax.all_to_all(values, GROUP, split_axis=0, concat_axis=0, tiled=True)


def norm(values, gain, axis):
    mean = jnp.mean(values, axis=axis, keepdims=True)
    centred = values - mean
    var = jnp.mean(centred * centred, axis=axis, keepdims=True)
    return centred * lax.rsqrt(var + 1e-05) * gain


def turned(proj):
    return proj.astype(jnp.float32).T.astype(jnp.bfloat16)


def project_tile(pairs, keep, in_gain, slab_proj, gate_proj):
    normed = norm(pairs, in_gain, 1).astype(jnp.bfloat16)
    raw = lax.dot_general(
        slab_proj, normed, (((1,), (1,)), ((), ())), preferred_element_type=jnp.float32
    )
    hidden = raw.shape[0] // 4
    left = jax.nn.sigmoid(raw[:hidden]) * raw[hidden : 2 * hidden] * keep
    right = jax.nn.sigmoid(raw[2 * hidden : 3 * hidden]) * raw[3 * hidden :] * keep
    gate = jax.nn.sigmoid(
        lax.dot_general(
            normed, gate_proj, (((1,), (0,)), ((), ())), preferred_element_type=jnp.float32
        )
    )
    return left.astype(jnp.bfloat16), right.astype(jnp.bfloat16), gate


def finish_tile(pairs, gate, product, mid_gain, final):
    normed = norm(product, mid_gain, 0).astype(jnp.bfloat16)
    change = lax.dot_general(
        normed, final, (((0,), (0,)), ((), ())), preferred_element_type=jnp.float32
    )
    return (pairs + gate * change).astype(jnp.bfloat16)


def tiles(count, half):
    out = []
    for h, size in enumerate((half, count - half)):
        cut = (size // 128 + 1) // 2 * 128
        for start, stop in ((0, cut), (cut, size)):
            out.append((h, slice(start, stop), slice(h * half + start, h * half + stop)))
    return out


def first_kernel(half, pair, mask, in_gain, proj, both, gate, keep):
    rows, cols = mask.shape
    hidden = both.shape[0]
    for r in range(rows):
        keep[:, r * cols : (r + 1) * cols] = mask[r : r + 1, :].astype(jnp.float32)
    slab_proj = turned(proj[:, : 4 * hidden])
    gate_proj = proj[:, 4 * hidden :]
    for _, _, at in tiles(pair.shape[0], half):
        left, right, gated = project_tile(
            pair[at, :].astype(jnp.float32), keep[:, at], in_gain[:, :], slab_proj, gate_proj
        )
        both[:, 0, at] = left
        both[:, 1, at] = right
        gate[at, :] = gated


def middle_kernel(
    pair, keep, gate_in, product, mid_gain, final, in_gain, proj, both, gate, middle
):
    hidden = both.shape[0]
    slab_proj = turned(proj[:, : 4 * hidden])
    gate_proj = proj[:, 4 * hidden :]
    for h, lanes, at in tiles(pair.shape[0], product.shape[2]):
        new = finish_tile(
            pair[at, :].astype(jnp.float32),
            gate_in[at, :],
            product[:, h, lanes].astype(jnp.float32),
            mid_gain[:, :],
            final[:, :],
        )
        middle[at, :] = new
        left, right, gated = project_tile(
            new.astype(jnp.float32), keep[:, at], in_gain[:, :], slab_proj, gate_proj
        )
        both[:, 0, at] = left
        both[:, 1, at] = right
        gate[at, :] = gated


def last_kernel(pair, gate_in, product, mid_gain, final, updated):
    for h, lanes, at in tiles(pair.shape[0], product.shape[2]):
        updated[at, :] = finish_tile(
            pair[at, :].astype(jnp.float32),
            gate_in[at, :],
            product[:, h, lanes].astype(jnp.float32),
            mid_gain[:, :],
            final[:, :],
        )


def call(kernel, outs, *args):
    whole = pl.BlockSpec(memory_space=pltpu.VMEM)
    return pl.pallas_call(
        kernel,
        out_shape=[jax.ShapeDtypeStruct(shape, dtype) for shape, dtype in outs],
        in_specs=[whole] * len(args),
        out_specs=[whole] * len(outs),
    )(*args)


def products(both, incoming, rows, cols, chans):
    got = exchange(both)
    size = got.shape[0]
    planes = got.reshape(size // chans, chans, 2, rows, cols)
    planes = planes.transpose(2, 0, 3, 1, 4).reshape(2, size // chans * rows, chans * cols)
    product = jnp.einsum(
        "ki,kj->ij" if incoming else "ik,jk->ij",
        planes[0],
        planes[1],
        preferred_element_type=jnp.float32,
    ).astype(jnp.bfloat16)
    parts = product.reshape(size // chans, rows, chans, cols).transpose(0, 2, 1, 3)
    tall = half_rows(rows)
    parts = jnp.pad(parts, ((0, 0), (0, 0), (0, 2 * tall - rows), (0, 0)))
    return exchange(parts.reshape(size, 2, tall * cols))


def half_rows(rows):
    return (rows + 15) // 16 * 8


def solution(mesh):
    chans = mesh.shape["chan"]

    def shards(
        pair,
        pair_mask,
        out_in_gain,
        out_proj,
        out_mid_gain,
        out_final,
        in_in_gain,
        in_proj,
        in_mid_gain,
        in_final,
    ):
        rows, cols, channels = pair.shape
        count = rows * cols
        hidden = out_final.shape[0]
        half = half_rows(rows) * cols
        pairs = pair.reshape(count, channels)
        slab_out = ((hidden, 2, count), jnp.bfloat16)
        gate_out = ((count, channels), jnp.float32)
        pair_out = ((count, channels), jnp.bfloat16)
        keep_out = ((1, count), jnp.float32)
        both, gate, keep = call(
            lambda *refs: first_kernel(half, *refs),
            [slab_out, gate_out, keep_out],
            pairs,
            pair_mask,
            out_in_gain[None],
            out_proj,
        )
        product = products(both, False, rows, cols, chans)
        both, gate, middle = call(
            middle_kernel,
            [slab_out, gate_out, pair_out],
            pairs,
            keep,
            gate,
            product,
            out_mid_gain[:, None],
            out_final,
            in_in_gain[None],
            in_proj,
        )
        product = products(both, True, rows, cols, chans)
        (updated,) = call(
            last_kernel, [pair_out], middle, gate, product, in_mid_gain[:, None], in_final
        )
        return updated.reshape(rows, cols, channels)

    placed = (
        P(("parts", "row", "sub"), "chan", None),
        P(("parts", "row", "sub"), "chan"),
    ) + (P(),) * 8
    return jax.shard_map(
        shards,
        mesh=mesh,
        in_specs=placed,
        out_specs=P(("parts", "row", "sub"), "chan", None),
        check_vma=False,
    )
```

time: 241 us -> 235 us (0.975)
  Pallas kernels: 0 us -> 13 us
  other arithmetic: 9.72 us -> 0 us
  matrix products: 6.19 us -> 0.85 us
  starting transfers between devices: 21.2 us -> 16.7 us
    pallas_call x0 -> x3, Pallas kernels: none -> 13 us  [call(): pl.pallas_call(kernel, out_shape=[jax.ShapeDtypeStruct(shape, dtype) for...]
    reduce_sum x7 -> x0, other arithmetic: 5.43 us -> none  [the longest x4 3.36 us: norm(): var = jnp.mean((values - mean) ** 2, axis=axis, keepdims=True)]
    dot_general x8 -> x2, matrix products: 6.19 us -> 0.85 us  [products(): jnp.einsum('ki,kj->ij' if incoming else 'ik,jk->ij', planes[0], planes[1]...]
    all_to_all x2, starting transfers between devices: 21.2 us -> 16.7 us  [exchange(): lax.all_to_all(values, GROUP, split_axis=0, concat_axis=0, tiled=True)]
    convert_element_type x4 -> x0, other arithmetic: 3.16 us -> none  [the longest x1 1.48 us: slabs(): normed = norm(pairs.astype(jnp.float32), in_gain, 1).astype(jnp.bfloat16)]
    unnamed x14 -> x8, local copies, waits for them, and re-layouts: 0.04 us -> 2.85 us
    another operation x2 -> x0, local copies, waits for them, and re-layouts: 2.57 us -> none  [slabs(): jnp.stack([left.astype(jnp.bfloat16), right.astype(jnp.bfloat16)], 1)]
where the time goes in v2:
time: 235 us; the launch traced here: 234 us
  blocking collectives  131 us (56%)
  waiting for transfers between devices  57 us (24%)
  starting transfers between devices  16.7 us (7%)
  local copies, waits for them, and re-layouts  15 us (6%)
  Pallas kernels  13 us (6%)
    all_to_all x2, blocking collectives, exchange(): lax.all_to_all(values, GROUP, split_axis=0, concat_axis=0, tiled=True)  131 us
    all_to_all x2, waiting for transfers between devices, exchange(): lax.all_to_all(values, GROUP, split_axis=0, concat_axis=0, tiled=True)  57 us
    all_to_all x2, starting transfers between devices, exchange(): lax.all_to_all(values, GROUP, split_axis=0, concat_axis=0, tiled=True)  16.7 us
    pallas_call x3, Pallas kernels, call(): pl.pallas_call(kernel, out_shape=[jax.ShapeDtypeStruct(shape, dtype) for...  13 us
  transfers between devices with their start and end apart: 2, of which 2 were waited for; matrix products, arithmetic and copies ran while one was open for 1% of the time, Pallas kernels for 0%

profile of v2, /device:TPU:33, one launch (start us, length us, event | category | flops | bytes accessed | tf_op | source)
XLA Modules:
  0.0 234.1 jit_solution(18399571703984895818)
XLA Ops:
  0.0 4.1 %shard_map.100 = (bf16[128,2,1568]{2,1,0:T(2,128)(2,1)}, f32[1568,128]{1,0:T(8,128)}, f32[1,1568]{1,0:T(1,128)}) custom-call(bf16[1568,128]{1,0:T(8,128)(2,1)} %bitcast.30, s32[14,112]{1,0:T(8,128)} %refs_1_.1, f32[1,128]{1,0:T(1,128)} %bitcast.34, bf16[128,640]{1,0:T(8,128)(2,1)} %refs_3_.1), custom_call_target="tpu_custom_call" | custom-call | tf_op jit(solution)/shard_map/pallas_call | solution.py:111
  4.1 77.2 %all_to_all.20 = bf16[128,2,1568]{2,1,0:T(2,128)(2,1)S(1)} all-to-all(bf16[128,2,1568]{2,1,0:T(2,128)(2,1)} %get-tuple-element.13), channel_id=1, replica_groups=mesh['parts'=2,'row'=16,'chan'=4,'sub'=2] {'row','sub','chan'}, dimensions={0} | all-to-all | bytes 1605632 | tf_op jit(solution)/shard_map/all_to_all | solution.py:12
  81.3 1.5 reshape.42
  82.8 0.3 copy.32
  83.1 0.2 fusion.1
  83.5 0.3 squeeze.12
  83.8 0.2 copy.17
  84.0 0.3 squeeze.13
  84.3 0.4 convolution_convert_fusion.1
  84.7 0.3 reshape.36
  85.3 1.9 reshape.37
  87.2 8.4 %all-to-all-start.1 = ((bf16[128,2,896]{2,1,0:T(2,128)(2,1)}), bf16[128,2,896]{2,1,0:T(2,128)(2,1)S(1)}, u32[]{:S(2)}, u32[]{:S(2)}) async-start(bf16[128,2,896]{2,1,0:T(2,128)(2,1)} %reshape.37), calls=%async_computation.1 | async-start | bytes 917504 | tf_op jit(solution)/shard_map/all_to_all | solution.py:12
  95.6 0.6 copy-done.2
  96.2 0.7 copy.19.mid_gain
  97.0 28.5 %all-to-all-done.1.product = bf16[128,2,896]{2,1,0:T(2,128)(2,1)S(1)} async-done(((bf16[128,2,896]{2,1,0:T(2,128)(2,1)}), bf16[128,2,896]{2,1,0:T(2,128)(2,1)S(1)}, u32[]{:S(2)}, u32[]{:S(2)}) %all-to-all-start.1) | async-done | bytes 458784 | tf_op jit(solution)/shard_map/all_to_all | solution.py:12
  125.5 0.8 copy-done.1
  126.2 5.8 %shard_map.101 = (bf16[128,2,1568]{2,1,0:T(2,128)(2,1)}, f32[1568,128]{1,0:T(8,128)}, bf16[1568,128]{1,0:T(8,128)(2,1)}) custom-call(bf16[1568,128]{1,0:T(8,128)(2,1)} %bitcast.31, f32[1,1568]{1,0:T(1,128)} %get-tuple-element.11.keep, f32[1568,128]{1,0:T(8,128)} %get-tuple-element.12.gate_in, bf16[128,2,896]{2,1,0:T(2,128)(2,1)} %copy-done.1, ...), custom_call_target="tpu_custom_call" | custom-call | tf_op jit(solution)/shard_map/pallas_call | solution.py:111
  132.1 54.2 %all_to_all.21 = bf16[128,2,1568]{2,1,0:T(2,128)(2,1)S(1)} all-to-all(bf16[128,2,1568]{2,1,0:T(2,128)(2,1)} %get-tuple-element.16), channel_id=1, replica_groups=mesh['parts'=2,'row'=16,'chan'=4,'sub'=2] {'row','sub','chan'}, dimensions={0} | all-to-all | bytes 1605632 | tf_op jit(solution)/shard_map/all_to_all | solution.py:12
  186.2 1.5 reshape.43
  187.7 0.3 copy.31
  188.0 0.2 fusion
  188.4 0.3 squeeze.14
  188.8 0.3 squeeze.15
  189.1 0.4 convolution_convert_fusion
  189.6 0.3 reshape.39
  190.2 1.9 reshape.40
  192.1 8.4 %all-to-all-start.3 = ((bf16[128,2,896]{2,1,0:T(2,128)(2,1)}), bf16[128,2,896]{2,1,0:T(2,128)(2,1)S(1)}, u32[]{:S(2)}, u32[]{:S(2)}) async-start(bf16[128,2,896]{2,1,0:T(2,128)(2,1)} %reshape.40), calls=%async_computation.3 | async-start | bytes 917504 | tf_op jit(solution)/shard_map/all_to_all | solution.py:12
  200.4 0.6 copy-done.3
  201.1 0.7 copy.24.mid_gain
  201.8 28.5 %all-to-all-done.3.product = bf16[128,2,896]{2,1,0:T(2,128)(2,1)S(1)} async-done(((bf16[128,2,896]{2,1,0:T(2,128)(2,1)}), bf16[128,2,896]{2,1,0:T(2,128)(2,1)S(1)}, u32[]{:S(2)}, u32[]{:S(2)}) %all-to-all-start.3) | async-done | bytes 458784 | tf_op jit(solution)/shard_map/all_to_all | solution.py:12
  230.3 0.8 copy-done
  231.1 3.0 %shard_map.102 = bf16[1568,128]{1,0:T(8,128)(2,1)} custom-call(bf16[1568,128]{1,0:T(8,128)(2,1)} %get-tuple-element.14.pair, f32[1568,128]{1,0:T(8,128)} %get-tuple-element.15.gate_in, bf16[128,2,896]{2,1,0:T(2,128)(2,1)} %copy-done, f32[128,1]{1,0:T(8,128)} %copy.24.mid_gain, bf16[128,128]{1,0:T(8,128)(2,1)} %final.3), custom_call_target="tpu_custom_call" | custom-call | tf_op jit(solution)/shard_map/pallas_call | solution.py:111
  (11 shorter events, 1.1 us)
Async XLA Ops:
  87.2 38.3 %all-to-all-start.1 = ((bf16[128,2,896]{2,1,0:T(2,128)(2,1)}), bf16[128,2,896]{2,1,0:T(2,128)(2,1)S(1)}, u32[]{:S(2)}, u32[]{:S(2)}) async-start(bf16[128,2,896]{2,1,0:T(2,128)(2,1)} %reshape.37), calls=%async_computation.1 | async-start | bytes 917504 | tf_op jit(solution)/shard_map/all_to_all | solution.py:12
  95.6 0.7 copy-start.2
  125.5 0.8 copy-start.1
  192.1 38.3 %all-to-all-start.3 = ((bf16[128,2,896]{2,1,0:T(2,128)(2,1)}), bf16[128,2,896]{2,1,0:T(2,128)(2,1)S(1)}, u32[]{:S(2)}, u32[]{:S(2)}) async-start(bf16[128,2,896]{2,1,0:T(2,128)(2,1)} %reshape.40), calls=%async_computation.3 | async-start | bytes 917504 | tf_op jit(solution)/shard_map/all_to_all | solution.py:12
  200.4 0.7 copy-start.3
  230.3 0.8 copy-start

commit v3 on v2

--- a/solution.py
+++ b/solution.py
@@ -37,6 +37,11 @@
         )
     )
     return left.astype(jnp.bfloat16), right.astype(jnp.bfloat16), gate
+
+
+def column(gain):
+    size = gain.shape[1]
+    return jnp.broadcast_to(gain, (size, size)).T[:, :1]
 
 
 def finish_tile(pairs, gate, product, mid_gain, final):
@@ -78,12 +83,13 @@
     hidden = both.shape[0]
     slab_proj = turned(proj[:, : 4 * hidden])
     gate_proj = proj[:, 4 * hidden :]
+    gain = column(mid_gain[:, :])
     for h, lanes, at in tiles(pair.shape[0], product.shape[2]):
         new = finish_tile(
             pair[at, :].astype(jnp.float32),
             gate_in[at, :],
             product[:, h, lanes].astype(jnp.float32),
-            mid_gain[:, :],
+            gain,
             final[:, :],
         )
         middle[at, :] = new
@@ -96,12 +102,13 @@
 
 
 def last_kernel(pair, gate_in, product, mid_gain, final, updated):
+    gain = column(mid_gain[:, :])
     for h, lanes, at in tiles(pair.shape[0], product.shape[2]):
         updated[at, :] = finish_tile(
             pair[at, :].astype(jnp.float32),
             gate_in[at, :],
             product[:, h, lanes].astype(jnp.float32),
-            mid_gain[:, :],
+            gain,
             final[:, :],
         )
 
@@ -177,14 +184,14 @@
             keep,
             gate,
             product,
-            out_mid_gain[:, None],
+            out_mid_gain[None],
             out_final,
             in_in_gain[None],
             in_proj,
         )
         product = products(both, True, rows, cols, chans)
         (updated,) = call(
-            last_kernel, [pair_out], middle, gate, product, in_mid_gain[:, None], in_final
+            last_kernel, [pair_out], middle, gate, product, in_mid_gain[None], in_final
         )
         return updated.reshape(rows, cols, channels)
 

time: 235 us -> 231 us (0.983)
  blocking collectives: 131 us -> 208 us
  waiting for transfers between devices: 57 us -> 0 us
  starting transfers between devices: 16.7 us -> 0 us
  local copies, waits for them, and re-layouts: 15 us -> 9.14 us
    all_to_all x2 -> x4, blocking collectives: 131 us -> 208 us  [exchange(): lax.all_to_all(values, GROUP, split_axis=0, concat_axis=0, tiled=True)]
    all_to_all x2 -> x0, waiting for transfers between devices: 57 us -> none  [exchange(): lax.all_to_all(values, GROUP, split_axis=0, concat_axis=0, tiled=True)]
    all_to_all x2 -> x0, starting transfers between devices: 16.7 us -> none  [exchange(): lax.all_to_all(values, GROUP, split_axis=0, concat_axis=0, tiled=True)]
    unnamed x8 -> x0, local copies, waits for them, and re-layouts: 2.85 us -> none
  transfers between devices with their start and end apart: 2 -> 0, of which waited for: 2 -> 0; matrix products, arithmetic and copies ran while one was open for 1% -> 0% of each run, Pallas kernels for 0% -> 0%
where the time goes in v3:
time: 231 us
  blocking collectives  208 us (90%)
  Pallas kernels  12.7 us (5%)
  local copies, waits for them, and re-layouts  9.14 us (4%)
    all_to_all x4, blocking collectives, exchange(): lax.all_to_all(values, GROUP, split_axis=0, concat_axis=0, tiled=True)  208 us
    pallas_call x3, Pallas kernels, call(): pl.pallas_call(kernel, out_shape=[jax.ShapeDtypeStruct(shape, dtype) for...  12.7 us

profile of v3, /device:TPU:33, one launch (start us, length us, event | category | flops | bytes accessed | tf_op | source)
XLA Modules:
  0.0 230.5 jit_solution(10345291393813478583)
XLA Ops:
  0.0 4.2 %shard_map.100 = (bf16[128,2,1568]{2,1,0:T(2,128)(2,1)}, f32[1568,128]{1,0:T(8,128)}, f32[1,1568]{1,0:T(1,128)}) custom-call(bf16[1568,128]{1,0:T(8,128)(2,1)} %bitcast.30, s32[14,112]{1,0:T(8,128)} %refs_1_.1, f32[1,128]{1,0:T(1,128)} %bitcast.35, bf16[128,640]{1,0:T(8,128)(2,1)} %refs_3_.1), custom_call_target="tpu_custom_call" | custom-call | tf_op jit(solution)/shard_map/pallas_call | solution.py:118
  4.2 77.2 %all_to_all.20 = bf16[128,2,1568]{2,1,0:T(2,128)(2,1)S(1)} all-to-all(bf16[128,2,1568]{2,1,0:T(2,128)(2,1)} %get-tuple-element.13), channel_id=1, replica_groups=mesh['parts'=2,'row'=16,'chan'=4,'sub'=2] {'row','sub','chan'}, dimensions={0} | all-to-all | bytes 1605632 | tf_op jit(solution)/shard_map/all_to_all | solution.py:12
  81.4 1.5 reshape.42
  82.8 0.3 copy.28
  83.1 0.2 fusion.1
  83.3 0.2 copy.15
  83.5 0.3 squeeze.13
  83.8 0.2 copy.14
  84.0 0.3 squeeze.12
  84.3 0.4 convolution_convert_fusion.1
  84.7 0.3 reshape.36
  85.1 0.1 copy.30
  85.2 0.1 pad.7
  85.3 1.1 reshape.37
  86.4 38.2 %all_to_all.21.product = bf16[128,2,896]{2,1,0:T(2,128)(2,1)} all-to-all(bf16[128,2,896]{2,1,0:T(2,128)(2,1)S(1)} %reshape.37), channel_id=1, replica_groups=mesh['parts'=2,'row'=16,'chan'=4,'sub'=2] {'row','sub','chan'}, dimensions={0} | all-to-all | bytes 917504 | tf_op jit(solution)/shard_map/all_to_all | solution.py:12
  124.6 5.5 %shard_map.101 = (bf16[128,2,1568]{2,1,0:T(2,128)(2,1)}, f32[1568,128]{1,0:T(8,128)}, bf16[1568,128]{1,0:T(8,128)(2,1)}) custom-call(bf16[1568,128]{1,0:T(8,128)(2,1)} %bitcast.31, f32[1,1568]{1,0:T(1,128)} %get-tuple-element.11.keep, f32[1568,128]{1,0:T(8,128)} %get-tuple-element.12.gate_in, bf16[128,2,896]{2,1,0:T(2,128)(2,1)} %all_to_all.21.product, ...), custom_call_target="tpu_custom_call" | custom-call | tf_op jit(solution)/shard_map/pallas_call | solution.py:118
  130.1 54.2 %all_to_all.22 = bf16[128,2,1568]{2,1,0:T(2,128)(2,1)S(1)} all-to-all(bf16[128,2,1568]{2,1,0:T(2,128)(2,1)} %get-tuple-element.16), channel_id=1, replica_groups=mesh['parts'=2,'row'=16,'chan'=4,'sub'=2] {'row','sub','chan'}, dimensions={0} | all-to-all | bytes 1605632 | tf_op jit(solution)/shard_map/all_to_all | solution.py:12
  184.2 1.5 reshape.43
  185.7 0.3 copy.27
  186.0 0.2 fusion
  186.2 0.2 copy.19
  186.4 0.3 squeeze.15
  186.7 0.2 copy.18
  186.9 0.3 squeeze.14
  187.2 0.4 convolution_convert_fusion
  187.6 0.3 reshape.39
  187.9 0.1 copy.29
  188.1 0.1 pad.8
  188.2 1.1 reshape.40
  189.3 38.2 %all_to_all.23.product = bf16[128,2,896]{2,1,0:T(2,128)(2,1)} all-to-all(bf16[128,2,896]{2,1,0:T(2,128)(2,1)S(1)} %reshape.40), channel_id=1, replica_groups=mesh['parts'=2,'row'=16,'chan'=4,'sub'=2] {'row','sub','chan'}, dimensions={0} | all-to-all | bytes 917504 | tf_op jit(solution)/shard_map/all_to_all | solution.py:12
  227.5 3.0 %shard_map.102 = bf16[1568,128]{1,0:T(8,128)(2,1)} custom-call(bf16[1568,128]{1,0:T(8,128)(2,1)} %get-tuple-element.14.pair, f32[1568,128]{1,0:T(8,128)} %get-tuple-element.15.gate_in, bf16[128,2,896]{2,1,0:T(2,128)(2,1)} %all_to_all.23.product, f32[1,128]{1,0:T(1,128)} %bitcast.34, bf16[128,128]{1,0:T(8,128)(2,1)} %final.3), custom_call_target="tpu_custom_call" | custom-call | tf_op jit(solution)/shard_map/pallas_call | solution.py:118

commit v4 on v3

--- a/solution.py
+++ b/solution.py
@@ -5,7 +5,7 @@
 from jax.experimental.pallas import tpu as pltpu
 from jax.sharding import PartitionSpec as P
 
-GROUP = ("row", "sub", "chan")
+GROUP = ("row", "chan", "sub")
 
 
 def exchange(values):
@@ -123,18 +123,19 @@
     )(*args)
 
 
-def products(both, incoming, rows, cols, chans):
+def products(both, incoming, rows, cols, chans, subs):
     got = exchange(both)
     size = got.shape[0]
-    planes = got.reshape(size // chans, chans, 2, rows, cols)
-    planes = planes.transpose(2, 0, 3, 1, 4).reshape(2, size // chans * rows, chans * cols)
+    planes = got.reshape(size // chans // subs, chans, subs, 2, rows, cols)
+    planes = planes.transpose(3, 0, 2, 4, 1, 5).reshape(2, size // chans * rows, chans * cols)
     product = jnp.einsum(
         "ki,kj->ij" if incoming else "ik,jk->ij",
         planes[0],
         planes[1],
         preferred_element_type=jnp.float32,
     ).astype(jnp.bfloat16)
-    parts = product.reshape(size // chans, rows, chans, cols).transpose(0, 2, 1, 3)
+    parts = product.reshape(size // chans // subs, subs, rows, chans, cols)
+    parts = parts.transpose(0, 3, 1, 2, 4).reshape(size // subs, subs, rows, cols)
     tall = half_rows(rows)
     parts = jnp.pad(parts, ((0, 0), (0, 0), (0, 2 * tall - rows), (0, 0)))
     return exchange(parts.reshape(size, 2, tall * cols))
@@ -145,7 +146,7 @@
 
 
 def solution(mesh):
-    chans = mesh.shape["chan"]
+    chans, subs = mesh.shape["chan"], mesh.shape["sub"]
 
     def shards(
         pair,
@@ -176,7 +177,7 @@
             out_in_gain[None],
             out_proj,
         )
-        product = products(both, False, rows, cols, chans)
+        product = products(both, False, rows, cols, chans, subs)
         both, gate, middle = call(
             middle_kernel,
             [slab_out, gate_out, pair_out],
@@ -189,7 +190,7 @@
             in_in_gain[None],
             in_proj,
         )
-        product = products(both, True, rows, cols, chans)
+        product = products(both, True, rows, cols, chans, subs)
         (updated,) = call(
             last_kernel, [pair_out], middle, gate, product, in_mid_gain[None], in_final
         )

time: 231 us -> 229 us (level)
  no operation moved by 1% of the time
where the time goes in v4:
time: 229 us
  blocking collectives  206 us (90%)
  Pallas kernels  12.7 us (6%)
  local copies, waits for them, and re-layouts  9.31 us (4%)
    all_to_all x4, blocking collectives, exchange(): lax.all_to_all(values, GROUP, split_axis=0, concat_axis=0, tiled=True)  206 us
    pallas_call x3, Pallas kernels, call(): pl.pallas_call(kernel, out_shape=[jax.ShapeDtypeStruct(shape, dtype) for...  12.7 us

profile of v4, /device:TPU:33, one launch (start us, length us, event | category | flops | bytes accessed | tf_op | source)
XLA Modules:
  0.0 229.0 jit_solution(8112275089281197449)
XLA Ops:
  0.0 4.2 %shard_map.100 = (bf16[128,2,1568]{2,1,0:T(2,128)(2,1)}, f32[1568,128]{1,0:T(8,128)}, f32[1,1568]{1,0:T(1,128)}) custom-call(bf16[1568,128]{1,0:T(8,128)(2,1)} %bitcast.30, s32[14,112]{1,0:T(8,128)} %refs_1_.1, f32[1,128]{1,0:T(1,128)} %bitcast.35, bf16[128,640]{1,0:T(8,128)(2,1)} %refs_3_.1), custom_call_target="tpu_custom_call" | custom-call | tf_op jit(solution)/shard_map/pallas_call | solution.py:118
  4.2 74.0 %all_to_all.20 = bf16[128,2,1568]{2,1,0:T(2,128)(2,1)S(1)} all-to-all(bf16[128,2,1568]{2,1,0:T(2,128)(2,1)} %get-tuple-element.13), channel_id=1, replica_groups=mesh['parts'=2,'row'=16,'chan'=4,'sub'=2] {'row','chan','sub'}, dimensions={0} | all-to-all | bytes 1605632 | tf_op jit(solution)/shard_map/all_to_all | solution.py:12
  78.2 1.5 reshape.50
  79.7 0.3 copy.26
  79.9 0.2 fusion.1
  80.2 0.2 copy.15
  80.4 0.3 squeeze.13
  80.7 0.2 copy.14
  80.9 0.3 squeeze.12
  81.2 0.4 convolution_convert_fusion.1
  81.7 0.3 reshape.42
  82.0 0.1 copy.16
  82.1 0.1 pad.7
  82.2 1.1 reshape.44
  83.3 39.3 %all_to_all.21.product = bf16[128,2,896]{2,1,0:T(2,128)(2,1)} all-to-all(bf16[128,2,896]{2,1,0:T(2,128)(2,1)S(1)} %reshape.44), channel_id=1, replica_groups=mesh['parts'=2,'row'=16,'chan'=4,'sub'=2] {'row','chan','sub'}, dimensions={0} | all-to-all | bytes 917504 | tf_op jit(solution)/shard_map/all_to_all | solution.py:12
  122.7 5.5 %shard_map.101 = (bf16[128,2,1568]{2,1,0:T(2,128)(2,1)}, f32[1568,128]{1,0:T(8,128)}, bf16[1568,128]{1,0:T(8,128)(2,1)}) custom-call(bf16[1568,128]{1,0:T(8,128)(2,1)} %bitcast.31, f32[1,1568]{1,0:T(1,128)} %get-tuple-element.11.keep, f32[1568,128]{1,0:T(8,128)} %get-tuple-element.12.gate_in, bf16[128,2,896]{2,1,0:T(2,128)(2,1)} %all_to_all.21.product, ...), custom_call_target="tpu_custom_call" | custom-call | tf_op jit(solution)/shard_map/pallas_call | solution.py:118
  128.1 53.3 %all_to_all.22 = bf16[128,2,1568]{2,1,0:T(2,128)(2,1)S(1)} all-to-all(bf16[128,2,1568]{2,1,0:T(2,128)(2,1)} %get-tuple-element.16), channel_id=1, replica_groups=mesh['parts'=2,'row'=16,'chan'=4,'sub'=2] {'row','chan','sub'}, dimensions={0} | all-to-all | bytes 1605632 | tf_op jit(solution)/shard_map/all_to_all | solution.py:12
  181.5 1.5 reshape.51
  182.9 0.3 copy.25
  183.2 0.2 fusion
  183.4 0.2 copy.19
  183.7 0.3 squeeze.15
  184.0 0.2 copy.18
  184.2 0.3 squeeze.14
  184.5 0.4 convolution_convert_fusion
  184.9 0.3 reshape.46
  185.3 0.1 copy.20
  185.4 0.1 pad.8
  185.5 1.1 reshape.48
  186.6 39.3 %all_to_all.23.product = bf16[128,2,896]{2,1,0:T(2,128)(2,1)} all-to-all(bf16[128,2,896]{2,1,0:T(2,128)(2,1)S(1)} %reshape.48), channel_id=1, replica_groups=mesh['parts'=2,'row'=16,'chan'=4,'sub'=2] {'row','chan','sub'}, dimensions={0} | all-to-all | bytes 917504 | tf_op jit(solution)/shard_map/all_to_all | solution.py:12
  225.9 3.0 %shard_map.102 = bf16[1568,128]{1,0:T(8,128)(2,1)} custom-call(bf16[1568,128]{1,0:T(8,128)(2,1)} %get-tuple-element.14.pair, f32[1568,128]{1,0:T(8,128)} %get-tuple-element.15.gate_in, bf16[128,2,896]{2,1,0:T(2,128)(2,1)} %all_to_all.23.product, f32[1,128]{1,0:T(1,128)} %bitcast.34, bf16[128,128]{1,0:T(8,128)(2,1)} %final.3), custom_call_target="tpu_custom_call" | custom-call | tf_op jit(solution)/shard_map/pallas_call | solution.py:118
